TPU v7x, 32 devices: a whole 2x2x4 slice. The times are simulated.
32 devices in a mesh: dp: 4 (over y, core), seq: 8 (over z, x).
Axes of the slice: x: 2, y: 2, z: 4, core: 2. Of those that a mesh axis runs over, the one named last changes fastest.
Arguments:
- queries: bfloat16 [4, 1024, 2048], P('dp', 'seq'), may hold values from -12 to 12
- keys: bfloat16 [4, 1024, 512], P('dp', 'seq'), may hold values from -4 to 4
- values: bfloat16 [4, 1024, 512], P('dp', 'seq'), may hold values from -6 to 6
- segments: int32 [4, 1024], P('dp', 'seq'), may hold values from 0 to 3, never falling along the last dimension, each value on 1 to 896 neighbouring positions
- task_ids: int32 [4], replicated, may hold values from 0 to 15
- prompt_keys: bfloat16 [16, 128, 512], P('seq'), may hold values from -4 to 4
- prompt_values: bfloat16 [16, 128, 512], P('seq'), may hold values from -6 to 6
- grad_out: bfloat16 [4, 1024, 2048], P('dp', 'seq'), may hold values from -6 to 6
Outputs:
- attended: bfloat16 [4, 1024, 2048], P('dp', 'seq')
- prompt_key_grad: float32 [16, 128, 512], P('seq')
- prompt_value_grad: float32 [16, 128, 512], P('seq')
Inputs may be any that keep to these rules, and one draw needn't show every extreme that they name: `segments`: along each example the document numbers never fall; one document holds 896 tokens.
All inputs are finite; a program needn't handle non-finite values.
Results may differ from a plain program's by a relative error of at most 0.0096.
Values may be sent and summed in bfloat16 or wider, within the bound.
A program may use at most 128 MiB of HBM per device.

v0:
```python
import math
import jax
import jax.numpy as jnp
from jax import lax
from jax.sharding import PartitionSpec as P

KVH = 4
GROUP = 4
HD = 128
PROMPT = 128


def spread(value, axis, source):
    kept = jnp.where(lax.axis_index(axis) == source, value, 0).astype(value.dtype)
    return lax.psum(kept, axis)


def shards(queries, keys, values, segments, task_ids, prompt_keys, prompt_values, grad_out):
    tok_rows = queries.shape[1]
    scaling = 1.0 / math.sqrt(HD)
    seq_rank = lax.axis_index("seq")
    query_heads = queries[0].reshape(tok_rows, KVH, GROUP, HD)
    query_segments = segments[0]
    query_index = seq_rank * tok_rows + lax.iota(jnp.int32, tok_rows)
    all_segments = lax.all_gather(segments[0], "seq", axis=0, tiled=True)
    bank_size = prompt_keys.shape[0]
    my_task = task_ids[lax.axis_index("dp")]
    prompt_owner = my_task // bank_size
    bank_slot = my_task % bank_size
    local_pair = jnp.stack(
        [
            lax.dynamic_index_in_dim(prompt_keys, bank_slot, 0, keepdims=False),
            lax.dynamic_index_in_dim(prompt_values, bank_slot, 0, keepdims=False),
        ]
    )
    shared_pair = spread(local_pair, "seq", prompt_owner)
    prompt_key_heads = shared_pair[0].reshape(PROMPT, KVH, HD)
    prompt_value_heads = shared_pair[1].reshape(PROMPT, KVH, HD)
    prompt_scores = (
        jnp.einsum(
            "tkgd,pkd->tkgp", query_heads, prompt_key_heads, preferred_element_type=jnp.float32
        )
        * scaling
    )
    maximum = jnp.max(prompt_scores, axis=-1)
    weights = jnp.exp(prompt_scores - maximum[..., None])
    totals = jnp.sum(weights, axis=-1)
    accumulated = jnp.einsum(
        "tkgp,pkd->tkgd",
        weights.astype(jnp.bfloat16),
        prompt_value_heads,
        preferred_element_type=jnp.float32,
    )
    carried = (maximum, totals, accumulated)

    def absorb_rows(state_now, stacked, first_row):
        key_count = stacked.shape[1]
        key_index = first_row + lax.iota(jnp.int32, key_count)
        key_segments = lax.dynamic_slice_in_dim(
            all_segments, jnp.maximum(first_row, 0), key_count, 0
        )
        key_mask = (
            (key_segments[None, :] == query_segments[:, None])
            & (key_index[None, :] <= query_index[:, None])
            & True
        )

        def update(inner_state):
            old_peak, old_totals, old_accum = inner_state
            key_heads = stacked[0].reshape(key_count, KVH, HD)
            value_heads = stacked[1].reshape(key_count, KVH, HD)
            scores = (
                jnp.einsum(
                    "tkgd,skd->tkgs", query_heads, key_heads, preferred_element_type=jnp.float32
                )
                * scaling
            )
            mask_wide = key_mask[:, None, None, :]
            new_peak = jnp.maximum(
                old_peak, jnp.max(jnp.where(mask_wide, scores, -jnp.inf), axis=-1)
            )
            shrink = jnp.exp(old_peak - new_peak)
            block_weights = jnp.where(mask_wide, jnp.exp(scores - new_peak[..., None]), 0.0)
            new_totals = old_totals * shrink + jnp.sum(block_weights, axis=-1)
            new_accum = old_accum * shrink[..., None] + jnp.einsum(
                "tkgs,skd->tkgd",
                block_weights.astype(jnp.bfloat16),
                value_heads,
                preferred_element_type=jnp.float32,
            )
            return (new_peak, new_totals, new_accum)

        return lax.cond(jnp.any(key_mask), update, lambda inner_state: inner_state, state_now)

    own_pair = jnp.stack([keys[0], values[0]])
    stacked = lax.all_gather(own_pair, "seq", axis=1, tiled=True)
    key_count = stacked.shape[1]
    tile_rows = 512

    def loop_tile(block_index, inner_state):
        offset = block_index * tile_rows
        piece = lax.dynamic_slice_in_dim(stacked, offset, tile_rows, 1)
        return absorb_rows(inner_state, piece, offset)

    carried = lax.fori_loop(0, key_count // tile_rows, loop_tile, carried)
    maximum, totals, accumulated = carried
    attended = (accumulated / totals[..., None]).astype(jnp.bfloat16)
    log_norm = maximum + jnp.log(totals)
    grad_heads = grad_out[0].reshape(tok_rows, KVH, GROUP, HD)
    attended_wide = lax.optimization_barrier(attended).astype(jnp.float32)
    row_delta = jnp.sum(grad_heads.astype(jnp.float32) * attended_wide, axis=-1)
    prompt_probs = jnp.exp(prompt_scores - log_norm[..., None])
    prompt_dots = jnp.einsum(
        "tkgd,pkd->tkgp", grad_heads, prompt_value_heads, preferred_element_type=jnp.float32
    )
    score_grad = prompt_probs * (prompt_dots - row_delta[..., None])
    value_part = jnp.einsum(
        "tkgp,tkgd->pkd",
        prompt_probs.astype(jnp.bfloat16),
        grad_heads,
        preferred_element_type=jnp.float32,
    )
    key_part = (
        jnp.einsum(
            "tkgp,tkgd->pkd",
            score_grad.astype(jnp.bfloat16),
            query_heads,
            preferred_element_type=jnp.float32,
        )
        * scaling
    )
    value_part = value_part.reshape(PROMPT, KVH * HD)
    key_part = key_part.reshape(PROMPT, KVH * HD)
    key_sum, value_sum = lax.psum((key_part, value_part), "seq")
    key_all, value_all = (
        lax.all_gather(key_sum[None].astype(jnp.bfloat16), "dp", axis=0, tiled=True).astype(
            jnp.float32
        ),
        lax.all_gather(value_sum[None].astype(jnp.bfloat16), "dp", axis=0, tiled=True).astype(
            jnp.float32
        ),
    )
    own_tasks = seq_rank * bank_size + lax.iota(jnp.int32, bank_size)
    matches = (task_ids[:, None] == own_tasks[None, :])[:, :, None, None]
    key_grad = jnp.sum(jnp.where(matches, key_all[:, None], 0.0), axis=0)
    value_grad = jnp.sum(jnp.where(matches, value_all[:, None], 0.0), axis=0)
    return (attended.reshape(1, tok_rows, KVH * GROUP * HD), key_grad, value_grad)


def solution(mesh):
    in_specs = (
        P("dp", "seq", None),
        P("dp", "seq", None),
        P("dp", "seq", None),
        P("dp", "seq"),
        P(),
        P("seq", None, None),
        P("seq", None, None),
        P("dp", "seq", None),
    )
    out_specs = (P("dp", "seq", None), P("seq", None, None), P("seq", None, None))
    return jax.shard_map(shards, mesh=mesh, in_specs=in_specs, out_specs=out_specs, check_vma=False)
```

profile of v0, /device:TPU:0, one launch (start us, length us, event | category | flops | bytes accessed | tf_op | source)
XLA Modules:
  0.0 223.2 jit_solution(11185119642300208240)
XLA Ops:
  7.2 1.3 dynamic_slice.28
  11.1 1.0 constant_dynamic-slice_fusion.2
  12.4 0.7 maximum_select_fusion
  13.2 1.0 copy.52
  14.3 1.0 copy.51
  15.3 0.7 pad_maximum_fusion
  16.0 1.3 copy.47
  17.9 22.3 %all-gather = s32[1,1024]{1,0:T(1,128)S(1)} all-gather(s32[1,128]{1,0:T(1,128)S(1)} %copy-done.3), channel_id=2, replica_groups=mesh['dp'=4,'seq'=8] {'seq'}, dimensions={1}, use_global_device_ids=true | all-gather | bytes 4608 | tf_op jit(solution)/shard_map/all_gather | solution.py:25
  40.3 46.8 %all-reduce.4.cloned.1.call-done = bf16[2,128,512]{1,2,0:T(8,128)(2,1)} async-done(((bf16[2,128,512]{1,2,0:T(8,128)(2,1)}), bf16[2,128,512]{1,2,0:T(8,128)(2,1)}) %all-reduce.4.cloned.1.call-update) | async-done | bytes 262160 | tf_op jit(solution)/shard_map/psum | solution.py:15
  87.1 1.0 fusion.39
  88.1 0.4 fusion.40
  88.4 1.3 convolution_bitcast_fusion.1
  89.7 2.5 %copy.53 = f32[128,4,4,128]{3,0,2,1:T(8,128)} copy(f32[128,4,4,128]{0,3,2,1:T(8,128)} %convolution_bitcast_fusion.1) | data formatting | bytes 2097152
  92.5 46.8 %all-gather.5.cloned.1.call-done = bf16[2,1024,512]{1,2,0:T(8,128)(2,1)} async-done(((bf16[2,128,512]{1,2,0:T(8,128)(2,1)}), bf16[2,1024,512]{1,2,0:T(8,128)(2,1)}) %all-gather.5.cloned.1.call-update) | async-done | bytes 2097168 | tf_op jit(solution)/shard_map/all_gather | solution.py:96
  139.3 8.8 %while.18 = (s32[]{:T(128)}, f32[128,4,4]{0,2,1:T(4,128)S(1)}, f32[128,4,4]{0,2,1:T(4,128)S(1)}, f32[128,4,4,128]{3,0,2,1:T(8,128)}, s32[1024]{0:T(1024)S(1)}, /...) while((s32[]{:T(128)}, f32[128,4,4]{0,2,1:T(4,128)S(1)}, ...), condition=%wide.region_9.10_spmd.clone, body=%wide.region_3.9_spmd.clone.sunk | while | flops 549196416 | bytes 27144068 | solution.py:105
  139.4 0.8 fusion.52
  140.8 5.6 %conditional.3 = ((f32[128,4,4]{0,2,1:T(4,128)S(1)}, f32[128,4,4]{0,2,1:T(4,128)S(1)}, f32[128,4,4,128]{3,0,2,1:T(8,128)})) conditional(s32[]{:T(128)} %convert_element_type.85, (f32[128,4,4]{0,2,1:T(4,128)S(1)}, f32[128,4,4]{0,2,1:T(4,128)S(1)}, f32[128,4,4,128]{3,0,2,1:T(8,128)}) %tuple.65, (pred[128,512]{0,1:T(8,128)(4,1)S(1)}, s32[]{:T(128)}, ...), branch_computations={%region_5.5_spmd, %region_6.8_spmd} | conditional | flops 548933632 | bytes 27066510 | solution.py:93
  140.9 1.3 constant_dynamic-slice_fusion.1
  142.2 0.9 fusion.2
  143.0 0.9 fusion.6
  143.9 1.5 fusion.16
  145.5 1.0 copy-done.1
  146.5 0.8 fusion.52
  148.0 2.6 %copy.55 = f32[128,4,4,128]{0,3,2,1:T(8,128)} copy(f32[128,4,4,128]{3,0,2,1:T(8,128)} %get-tuple-element.225) | data formatting | bytes 2097152 | tf_op jit(solution)/shard_map/while | solution.py:105
  150.6 1.3 divide_convert_fusion
  151.9 1.0 copy.63
  153.1 0.3 fusion.31
  153.4 0.6 fusion.27
  154.0 45.7 %all-reduce.5 = (bf16[128,512]{0,1:T(8,128)(2,1)S(1)}, bf16[128,512]{0,1:T(8,128)(2,1)S(1)}) all-reduce(f32[128,512]{0,1:T(8,128)S(1)} %bitcast.123, f32[128,512]{0,1:T(8,128)S(1)} %bitcast.122), channel_id=1, replica_groups=mesh['dp'=4,'seq'=8] {'seq'}, use_global_device_ids=true, to_apply=%region_11.12 | all-reduce | flops 131072 | bytes 786432 | tf_op jit(solution)/shard_map/psum | solution.py:134
  199.7 7.6 %all-gather.2 = bf16[512,512]{0,1:T(8,128)(2,1)S(1)} all-gather(bf16[128,512]{0,1:T(8,128)(2,1)S(1)} %get-tuple-element.306), channel_id=4, replica_groups=mesh['dp'=4,'seq'=8] {'dp'}, dimensions={0}, use_global_device_ids=true | all-gather | bytes 655360 | tf_op jit(solution)/shard_map/all_gather | solution.py:139
  207.5 7.3 %all-gather.1 = bf16[512,512]{0,1:T(8,128)(2,1)S(1)} all-gather(bf16[128,512]{0,1:T(8,128)(2,1)S(1)} %get-tuple-element.305), channel_id=3, replica_groups=mesh['dp'=4,'seq'=8] {'dp'}, dimensions={0}, use_global_device_ids=true | all-gather | bytes 655360 | tf_op jit(solution)/shard_map/all_gather | solution.py:136
  215.0 1.3 select_reduce_fusion
  (34 shorter events, 2.0 us)
Async XLA Ops:
  7.2 33.1 %copy-start.4 = (s32[4]{0:T(128)S(1)}, s32[4]{0:T(128)}, u32[]{:S(2)}) copy-start(s32[4]{0:T(128)} %param.16) | copy-start | bytes 52
  7.2 10.5 %copy-start.2 = (bf16[1,128,2048]{2,1,0:T(8,128)(2,1)S(1)}, bf16[1,128,2048]{2,1,0:T(8,128)(2,1)}, u32[]{:S(2)}) copy-start(bf16[1,128,2048]{2,1,0:T(8,128)(2,1)} %param.19) | copy-start | bytes 1572868
  7.2 10.8 %copy-start.3 = (s32[1,128]{1,0:T(1,128)S(1)}, s32[1,128]{1,0:T(1,128)}, u32[]{:S(2)}) copy-start(s32[1,128]{1,0:T(1,128)} %param.15) | copy-start | bytes 1540
  7.2 79.9 %all-reduce.4.cloned.1.call-start = ((), (), s32[]{:S(2)}) async-start(), calls=%async_computation | async-start | bytes 524288 | tf_op jit(solution)/shard_map/psum | solution.py:15
  13.2 126.1 %all-gather.5.cloned.1.call-start = ((), (), s32[]{:S(2)}) async-start(), calls=%async_computation.1 | async-start | bytes 2359296 | tf_op jit(solution)/shard_map/all_gather | solution.py:96
  142.1 1.8 copy-start
  145.4 1.0 copy-start.1
Sparse Core Ops, SparseCore 0:
  13.3 73.7 all-reduce.3
  89.7 49.5 all-gather.4
where the time goes:
time: 224 us; the launch traced here: 223 us
  waiting for transfers between devices  93.6 us (42%)
  blocking collectives  82.9 us (37%)
  between operations  16.8 us (8%)
  local copies, waits for them, and re-layouts  16.4 us (7%)
  other arithmetic  7.1 us (3%)
  matrix products  4.91 us (2%)
    all_gather x1, waiting for transfers between devices, shards(): stacked = lax.all_gather(own_pair, 'seq', axis=1, tiled=True)  46.8 us
    psum x1, waiting for transfers between devices, spread(): return lax.psum(kept, axis)  46.8 us
    psum x1, blocking collectives, shards(): key_sum, value_sum = lax.psum((key_part, value_part), 'seq')  45.7 us
    all_gather x1, blocking collectives, shards(): all_segments = lax.all_gather(segments[0], 'seq', axis=0, tiled=True)  22.3 us
    unnamed x15, local copies, waits for them, and re-layouts  7.72 us
    all_gather x1, blocking collectives, shards(): lax.all_gather(value_sum[None].astype(jnp.bfloat16), 'dp', axis=0, tiled=...  7.59 us
    all_gather x1, blocking collectives, shards(): lax.all_gather(key_sum[None].astype(jnp.bfloat16), 'dp', axis=0, tiled=True)  7.3 us
  transfers between devices with their start and end apart: 2, of which 2 were waited for; matrix products, arithmetic and copies ran while one was open for 5% of the time, Pallas kernels for 0%

commit v1 on v0

--- a/solution.py
+++ b/solution.py
@@ -12,7 +12,7 @@
 
 def spread(value, axis, source):
     kept = jnp.where(lax.axis_index(axis) == source, value, 0).astype(value.dtype)
-    return lax.psum(kept, axis)
+    return jnp.sum(lax.all_gather(kept, axis), axis=0)
 
 
 def shards(queries, keys, values, segments, task_ids, prompt_keys, prompt_values, grad_out):

time: 224 us -> 201 us (0.90)
  waiting for transfers between devices: 93.6 us -> 69.7 us
    psum x1 -> x0, waiting for transfers between devices: 46.8 us -> none  [spread(): return lax.psum(kept, axis)]
    all_gather x0 -> x1, waiting for transfers between devices: none -> 24.8 us  [spread(): return jnp.sum(lax.all_gather(kept, axis), axis=0)]
    unnamed x15 -> x13, local copies, waits for them, and re-layouts: 7.72 us -> 7.49 us
  transfers between devices with their start and end apart: 2 -> 2, of which waited for: 2 -> 2; matrix products, arithmetic and copies ran while one was open for 5% -> 6% of each run, Pallas kernels for 0% -> 0%
where the time goes in v1:
time: 201 us; the launch traced here: 200 us
  blocking collectives  83 us (41%)
  waiting for transfers between devices  69.7 us (35%)
  between operations  16.8 us (8%)
  local copies, waits for them, and re-layouts  15.4 us (8%)
  other arithmetic  9.06 us (5%)
  matrix products  4.92 us (2%)
    psum x1, blocking collectives, shards(): key_sum, value_sum = lax.psum((key_part, value_part), 'seq')  45.7 us
    all_gather x1, waiting for transfers between devices, shards(): stacked = lax.all_gather(own_pair, 'seq', axis=1, tiled=True)  44.9 us
    all_gather x1, waiting for transfers between devices, spread(): return jnp.sum(lax.all_gather(kept, axis), axis=0)  24.8 us
    all_gather x1, blocking collectives, shards(): all_segments = lax.all_gather(segments[0], 'seq', axis=0, tiled=True)  22.4 us
    all_gather x1, blocking collectives, shards(): lax.all_gather(value_sum[None].astype(jnp.bfloat16), 'dp', axis=0, tiled=...  7.59 us
    unnamed x13, local copies, waits for them, and re-layouts  7.49 us
    all_gather x1, blocking collectives, shards(): lax.all_gather(key_sum[None].astype(jnp.bfloat16), 'dp', axis=0, tiled=True)  7.3 us
  transfers between devices with their start and end apart: 2, of which 2 were waited for; matrix products, arithmetic and copies ran while one was open for 6% of the time, Pallas kernels for 0%

profile of v1, /device:TPU:0, one launch (start us, length us, event | category | flops | bytes accessed | tf_op | source)
XLA Modules:
  0.0 200.4 jit_solution(16342345893021731642)
XLA Ops:
  7.2 1.3 dynamic_slice.28
  11.2 1.0 dynamic-slice_bitcast_fusion
  12.2 0.7 maximum_select_fusion
  13.0 1.0 copy.71
  14.0 1.0 copy.70
  15.0 0.7 pad_maximum_fusion
  15.8 1.3 copy.65
  17.7 22.4 %all-gather = s32[1,1024]{1,0:T(1,128)S(1)} all-gather(s32[1,128]{1,0:T(1,128)S(1)} %copy-done.3), channel_id=2, replica_groups=mesh['dp'=4,'seq'=8] {'seq'}, dimensions={1}, use_global_device_ids=true | all-gather | bytes 4608 | tf_op jit(solution)/shard_map/all_gather | solution.py:25
  40.2 24.8 %all-gather.6.cloned.1.call-done = bf16[8,2,128,512]{3,2,1,0:T(8,128)(2,1)} async-done(((bf16[1,2,128,512]{3,2,1,0:T(8,128)(2,1)}), bf16[8,2,128,512]{3,2,1,0:T(8,128)(2,1)}) %all-gather.6.cloned.1.call-update) | async-done | bytes 2097168 | tf_op jit(solution)/shard_map/all_gather | solution.py:15
  64.9 2.0 reduce_sum.58
  67.2 0.4 fusion.40
  67.6 1.3 convolution_bitcast_fusion.1
  68.9 2.5 %copy.72 = f32[128,4,4,128]{3,0,2,1:T(8,128)} copy(f32[128,4,4,128]{0,3,2,1:T(8,128)} %convolution_bitcast_fusion.1) | data formatting | bytes 2097152
  71.6 44.9 %all-gather.8.cloned.1.call-done = bf16[2,1024,512]{1,2,0:T(8,128)(2,1)} async-done(((bf16[2,128,512]{1,2,0:T(8,128)(2,1)}), bf16[2,1024,512]{1,2,0:T(8,128)(2,1)}) %all-gather.8.cloned.1.call-update) | async-done | bytes 2097168 | tf_op jit(solution)/shard_map/all_gather | solution.py:96
  116.5 8.8 %while.18 = (s32[]{:T(128)}, f32[128,4,4]{0,2,1:T(4,128)S(1)}, f32[128,4,4]{0,2,1:T(4,128)S(1)}, f32[128,4,4,128]{3,0,2,1:T(8,128)}, s32[1024]{0:T(1024)S(1)}, /...) while((s32[]{:T(128)}, f32[128,4,4]{0,2,1:T(4,128)S(1)}, ...), condition=%wide.region_9.10_spmd.clone, body=%wide.region_3.9_spmd.clone.sunk | while | flops 549196416 | bytes 27144068 | solution.py:105
  116.5 0.8 fusion.52
  118.0 5.6 %conditional.3 = ((f32[128,4,4]{0,2,1:T(4,128)S(1)}, f32[128,4,4]{0,2,1:T(4,128)S(1)}, f32[128,4,4,128]{3,0,2,1:T(8,128)})) conditional(s32[]{:T(128)} %convert_element_type.87, (f32[128,4,4]{0,2,1:T(4,128)S(1)}, f32[128,4,4]{0,2,1:T(4,128)S(1)}, f32[128,4,4,128]{3,0,2,1:T(8,128)}) %tuple.67, (pred[128,512]{0,1:T(8,128)(4,1)S(1)}, s32[]{:T(128)}, ...), branch_computations={%region_5.5_spmd, %region_6.8_spmd} | conditional | flops 548933632 | bytes 27066510 | solution.py:93
  118.1 1.3 constant_dynamic-slice_fusion.1
  119.3 0.9 fusion.2
  120.2 0.9 fusion.6
  121.1 1.5 fusion.16
  122.6 1.0 copy-done.1
  123.7 0.8 fusion.52
  125.2 2.6 %copy.74 = f32[128,4,4,128]{0,3,2,1:T(8,128)} copy(f32[128,4,4,128]{3,0,2,1:T(8,128)} %get-tuple-element.225) | data formatting | bytes 2097152 | tf_op jit(solution)/shard_map/while | solution.py:105
  127.8 1.3 divide_convert_fusion
  129.1 1.0 copy.82
  130.3 0.3 fusion.31
  130.6 0.6 fusion.27
  131.2 45.7 %all-reduce.2 = (bf16[128,512]{0,1:T(8,128)(2,1)S(1)}, bf16[128,512]{0,1:T(8,128)(2,1)S(1)}) all-reduce(f32[128,512]{0,1:T(8,128)S(1)} %bitcast.127, f32[128,512]{0,1:T(8,128)S(1)} %bitcast.126), channel_id=1, replica_groups=mesh['dp'=4,'seq'=8] {'seq'}, use_global_device_ids=true, to_apply=%region_11.12 | all-reduce | flops 131072 | bytes 786432 | tf_op jit(solution)/shard_map/psum | solution.py:134
  176.9 7.6 %all-gather.2 = bf16[512,512]{0,1:T(8,128)(2,1)S(1)} all-gather(bf16[128,512]{0,1:T(8,128)(2,1)S(1)} %get-tuple-element.318), channel_id=4, replica_groups=mesh['dp'=4,'seq'=8] {'dp'}, dimensions={0}, use_global_device_ids=true | all-gather | bytes 655360 | tf_op jit(solution)/shard_map/all_gather | solution.py:139
  184.7 7.3 %all-gather.1 = bf16[512,512]{0,1:T(8,128)(2,1)S(1)} all-gather(bf16[128,512]{0,1:T(8,128)(2,1)S(1)} %get-tuple-element.317), channel_id=3, replica_groups=mesh['dp'=4,'seq'=8] {'dp'}, dimensions={0}, use_global_device_ids=true | all-gather | bytes 655360 | tf_op jit(solution)/shard_map/all_gather | solution.py:136
  192.2 1.3 select_reduce_fusion
  (35 shorter events, 2.0 us)
Async XLA Ops:
  7.2 32.9 %copy-start.4 = (s32[4]{0:T(128)S(1)}, s32[4]{0:T(128)}, u32[]{:S(2)}) copy-start(s32[4]{0:T(128)} %param.16) | copy-start | bytes 52
  7.2 10.2 %copy-start.2 = (bf16[1,128,2048]{2,1,0:T(8,128)(2,1)S(1)}, bf16[1,128,2048]{2,1,0:T(8,128)(2,1)}, u32[]{:S(2)}) copy-start(bf16[1,128,2048]{2,1,0:T(8,128)(2,1)} %param.19) | copy-start | bytes 1572868
  7.2 10.5 %copy-start.3 = (s32[1,128]{1,0:T(1,128)S(1)}, s32[1,128]{1,0:T(1,128)}, u32[]{:S(2)}) copy-start(s32[1,128]{1,0:T(1,128)} %param.15) | copy-start | bytes 1540
  7.2 57.7 %all-gather.6.cloned.1.call-start = ((), (), s32[]{:S(2)}) async-start(), calls=%async_computation | async-start | bytes 2359296 | tf_op jit(solution)/shard_map/all_gather | solution.py:15
  12.9 103.5 %all-gather.8.cloned.1.call-start = ((), (), s32[]{:S(2)}) async-start(), calls=%async_computation.1 | async-start | bytes 2359296 | tf_op jit(solution)/shard_map/all_gather | solution.py:96
  119.3 1.8 copy-start
  122.6 1.0 copy-start.1
Sparse Core Ops, SparseCore 0:
  13.0 51.8 all-gather.5
  67.5 48.8 all-gather.7
